TPU v7x, 32 devices: a whole 2x2x4 slice. The times are simulated.
32 devices in a mesh: tensor: 2 (over x), context: 8 (over z, core), dp: 2 (over y).
Axes of the slice: x: 2, y: 2, z: 4, core: 2. Of those that a mesh axis runs over, the one named last changes fastest.
Arguments:
- query_a: bfloat16 [2048, 1024], P(('dp', 'context'), 'tensor'), parts along dimension 0, may hold values from -5 to 5
- key_a: bfloat16 [2048, 256], P(('dp', 'context'), 'tensor'), parts along dimension 0, may hold values from -5 to 5
- value_a: bfloat16 [2048, 256], P(('dp', 'context'), 'tensor'), parts along dimension 0, may hold values from -12 to 12
- grad_out_a: bfloat16 [2048, 1024], P(('dp', 'context'), 'tensor'), parts along dimension 0, may hold values from -6 to 6
- query_b: bfloat16 [2048, 1024], P(('dp', 'context'), 'tensor'), parts along dimension 0, may hold values from -5 to 5
- key_b: bfloat16 [2048, 256], P(('dp', 'context'), 'tensor'), parts along dimension 0, may hold values from -5 to 5
- value_b: bfloat16 [2048, 256], P(('dp', 'context'), 'tensor'), parts along dimension 0, may hold values from -12 to 12
- slab_owner: int32 [8], replicated, may hold values from 0 to 7, each once
Outputs:
- out_b: bfloat16 [2048, 1024], P(('dp', 'context'), 'tensor'), parts along dimension 0
- grad_query_a: bfloat16 [2048, 1024], P(('dp', 'context'), 'tensor'), parts along dimension 0
- grad_key_a: bfloat16 [2048, 256], P(('dp', 'context'), 'tensor'), parts along dimension 0
- grad_value_a: bfloat16 [2048, 256], P(('dp', 'context'), 'tensor'), parts along dimension 0
There are 2 independent parts, one for each index of `dp`. A program takes and returns all parts, laid end to end along the dimension named above; an argument that names none is the same for every part. Nothing has to cross between parts.
Inputs may be any that keep to these rules, and one draw needn't show every extreme that they name: `slab_owner`: each number appears once.
All inputs are finite; a program needn't handle non-finite values.
Results may differ from a plain program's by a relative error of at most 0.0091.
Values may be sent and summed in bfloat16 or wider, within the bound.
A program may use at most 64 MiB of HBM per device.

v0:
```python
from functools import partial
import math

import jax
import jax.numpy as jnp
from jax import lax
from jax.sharding import PartitionSpec as P

masked_low = -1e30


def slab_places(slab_owner, first_row, row_count, tok_rows):
    half = tok_rows // 2
    devices = slab_owner.shape[0]
    rows = first_row + jnp.arange(row_count, dtype=jnp.int32)
    holder = rows // tok_rows
    within = rows % tok_rows
    ranks = jnp.arange(devices, dtype=jnp.int32)
    owner_slab = jnp.sum(
        jnp.where(holder[:, None] == ranks[None, :], slab_owner[None, :], 0), axis=1
    )
    slab = jnp.where(within < half, owner_slab, 2 * devices - 1 - owner_slab)
    return slab * half + within % half


def scores_of(queries, keys, query_places, key_places):
    scale = keys.shape[1] ** (-0.5)
    raw = jnp.einsum("rhd,nd->hrn", queries, keys, preferred_element_type=jnp.float32)
    allowed = key_places[None, None, :] <= query_places[None, :, None]
    return (raw * scale, allowed)


def over_rows(advance, carried, pieces, first_row):
    row_count = pieces[0].shape[0]
    block_rows = math.gcd(row_count, 512)

    def one_block(index, state):
        offset = index * block_rows
        portion = tuple(
            (lax.dynamic_slice_in_dim(piece, offset, block_rows, 0) for piece in pieces)
        )
        return advance(state, portion, first_row + offset)

    return lax.fori_loop(0, row_count // block_rows, one_block, carried)


def attend(queries, query_places, slab_owner, tok_rows, state, pieces, first_row):
    top, total, summed = state
    keys, values = pieces
    key_places = slab_places(slab_owner, first_row, keys.shape[0], tok_rows)
    scaled, allowed = scores_of(queries, keys, query_places, key_places)
    new_top = jnp.maximum(top, jnp.max(jnp.where(allowed, scaled, masked_low), axis=2))
    raised = jnp.where(allowed, jnp.exp(scaled - new_top[:, :, None]), 0.0)
    factor = jnp.exp(top - new_top)
    total = total * factor + jnp.sum(raised, axis=2)
    added = jnp.einsum(
        "hrn,nd->rhd", raised.astype(jnp.bfloat16), values, preferred_element_type=jnp.float32
    )
    summed = summed * jnp.transpose(factor)[:, :, None] + added
    return (new_top, total, summed)


def finish(state):
    return state[2] / jnp.transpose(state[1])[:, :, None]


def grad_terms(queries, grads, query_places, log_total, delta, keys, values, key_places):
    scaled, allowed = scores_of(queries, keys, query_places, key_places)
    prob = jnp.where(allowed, jnp.exp(scaled - log_total[:, :, None]), 0.0)
    prob_grad = jnp.einsum("rhd,nd->hrn", grads, values, preferred_element_type=jnp.float32)
    score_grad = (prob * (prob_grad - delta[:, :, None])).astype(jnp.bfloat16)
    return (prob.astype(jnp.bfloat16), score_grad)


def on_device(query_a, key_a, value_a, grad_out_a, query_b, key_b, value_b, slab_owner):
    tok_rows = query_a.shape[0]
    head_dim = key_a.shape[1]
    heads = query_a.shape[1] // head_dim
    scale = head_dim ** (-0.5)
    here = lax.axis_index("context")
    own_places = slab_places(slab_owner, here * tok_rows, tok_rows, tok_rows)
    queries_a = query_a.reshape(tok_rows, heads, head_dim)
    queries_b = query_b.reshape(tok_rows, heads, head_dim)
    grads_a = grad_out_a.reshape(tok_rows, heads, head_dim)
    start_state = (
        jnp.full((heads, tok_rows), masked_low, jnp.float32),
        jnp.zeros((heads, tok_rows), jnp.float32),
        jnp.zeros((tok_rows, heads, head_dim), jnp.float32),
    )
    advance_a = partial(attend, queries_a, own_places, slab_owner, tok_rows)
    advance_b = partial(attend, queries_b, own_places, slab_owner, tok_rows)
    all_keys, all_values, keys_b, values_b = (
        lax.all_gather(key_a, "context", axis=0, tiled=True),
        lax.all_gather(value_a, "context", axis=0, tiled=True),
        lax.all_gather(key_b, "context", axis=0, tiled=True),
        lax.all_gather(value_b, "context", axis=0, tiled=True),
    )
    state_b = over_rows(advance_b, start_state, (keys_b, values_b), 0)
    out_b = finish(state_b).reshape(tok_rows, heads * head_dim).astype(jnp.bfloat16)
    state_a = over_rows(advance_a, start_state, (all_keys, all_values), 0)
    mixed_a = finish(state_a)
    log_total = state_a[0] + jnp.log(state_a[1])
    delta = jnp.transpose(jnp.sum(grads_a.astype(jnp.float32) * mixed_a, axis=2))

    def query_step(state, pieces, first_row):
        keys, values = pieces
        key_places = slab_places(slab_owner, first_row, keys.shape[0], tok_rows)
        score_grad = grad_terms(
            queries_a, grads_a, own_places, log_total, delta, keys, values, key_places
        )[1]
        return state + jnp.einsum(
            "hrn,nd->rhd", score_grad, keys, preferred_element_type=jnp.float32
        )

    query_sum = over_rows(
        query_step, jnp.zeros((tok_rows, heads, head_dim), jnp.float32), (all_keys, all_values), 0
    )
    grad_query_a = (query_sum * scale).reshape(tok_rows, heads * head_dim).astype(jnp.bfloat16)
    keys = all_keys
    values = all_values

    def advance(term, pieces, row_start):
        block_keys, block_values = pieces
        key_places = slab_places(slab_owner, row_start, block_keys.shape[0], tok_rows)
        low_prob, score_grad = grad_terms(
            queries_a, grads_a, own_places, log_total, delta, block_keys, block_values, key_places
        )
        key_part = jnp.einsum(
            "hrn,rhd->nd", score_grad, queries_a, preferred_element_type=jnp.float32
        )
        value_part = jnp.einsum(
            "hrn,rhd->nd", low_prob, grads_a, preferred_element_type=jnp.float32
        )
        joined = jnp.concatenate([key_part, value_part], axis=1)
        return lax.dynamic_update_slice_in_dim(term, joined, row_start, 0)

    blank = jnp.zeros((tok_rows * lax.axis_size("context"), 2 * head_dim), jnp.float32)
    terms = lax.psum_scatter(
        over_rows(advance, blank, (keys, values), jnp.int32(0)),
        "context",
        scatter_dimension=0,
        tiled=True,
    )
    key_sum = terms[:, :head_dim]
    value_sum = terms[:, head_dim:]
    grad_key_a = (key_sum * scale).astype(jnp.bfloat16)
    grad_value_a = value_sum.astype(jnp.bfloat16)
    return (out_b, grad_query_a, grad_key_a, grad_value_a)


def solution(mesh):
    placed = (
        P(("dp", "context"), "tensor"),
        P(("dp", "context"), "tensor"),
        P(("dp", "context"), "tensor"),
        P(("dp", "context"), "tensor"),
        P(("dp", "context"), "tensor"),
        P(("dp", "context"), "tensor"),
        P(("dp", "context"), "tensor"),
        P(),
    )
    return jax.shard_map(
        on_device,
        mesh=mesh,
        in_specs=placed,
        out_specs=(
            P(("dp", "context"), "tensor"),
            P(("dp", "context"), "tensor"),
            P(("dp", "context"), "tensor"),
            P(("dp", "context"), "tensor"),
        ),
        check_vma=False,
    )
```

profile of v0, /device:TPU:0, one launch (start us, length us, event | category | flops | bytes accessed | tf_op | source)
XLA Modules:
  0.0 91.6 jit_solution(16200788325912349170)
XLA Ops:
  7.3 0.6 copy-done.1
  8.0 16.1 %all_gather.14 = bf16[1024,128]{1,0:T(8,128)(2,1)S(1)} all-gather(bf16[128,128]{1,0:T(8,128)(2,1)} %param.17), channel_id=1, replica_groups=mesh['tensor'=2,'context'=8,'dp'=2] {'context'}, dimensions={0}, use_global_device_ids=true | all-gather | bytes 294912 | tf_op jit(solution)/shard_map/all_gather | solution.py:93
  24.2 14.3 %all_gather.15 = bf16[1024,128]{1,0:T(8,128)(2,1)S(1)} all-gather(bf16[128,128]{1,0:T(8,128)(2,1)S(1)} %copy-done.5), channel_id=1, replica_groups=mesh['tensor'=2,'context'=8,'dp'=2] {'context'}, dimensions={0}, use_global_device_ids=true | all-gather | bytes 294912 | tf_op jit(solution)/shard_map/all_gather | solution.py:94
  38.7 2.5 %while.77 = (s32[]{:T(128)}, f32[4,128]{1,0:T(4,128)S(1)}, f32[4,128]{1,0:T(4,128)S(1)}, f32[128,4,128]{0,2,1:T(8,128)S(1)}, s32[8]{0:T(128)S(1)}, /*index=5*/s3...) while((s32[]{:T(128)}, f32[4,128]{1,0:T(4,128)S(1)}, ...), condition=%wide.region_10.11_spmd.clone, body=%wide.region_6.10_spmd.clone.sunk | while | flops 136876544 | bytes 4371175 | solution.py:44
  39.4 0.4 fusion.173
  40.6 0.4 fusion.173
  41.7 3.6 %while.75 = (s32[]{:T(128)}, f32[1024,256]{1,0:T(8,128)S(1)}, s32[8]{0:T(128)S(1)}, s32[128]{0:T(128)S(1)}, bf16[1024,128]{1,0:T(8,128)(2,1)S(1)}, /*index=5*/bf...) while((s32[]{:T(128)}, f32[1024,256]{1,0:T(8,128)S(1)}, ...), condition=%wide.region_17.18_spmd, body=%wide.region_15.17_spmd.sunk | while | flops 270501376 | bytes 7750375 | solution.py:44
  42.3 0.5 fusion.157
  44.1 0.5 fusion.157
  45.3 0.6 copy-done.8
  45.9 0.4 copy-done
  46.5 0.7 copy-done.9
  47.2 2.5 %while.78 = (s32[]{:T(128)}, f32[128,4,128]{0,2,1:T(8,128)S(1)}, bf16[1024,128]{1,0:T(8,128)(2,1)S(1)}, s32[8]{0:T(128)S(1)}, s32[128]{0:T(128)S(1)}, /*index=5*...) while((s32[]{:T(128)}, f32[128,4,128]{0,2,1:T(8,128)S(1)}, ...), condition=%wide.region_14.15_spmd.clone, body=%wide.region_12.14_spmd.clone.sunk | while | flops 203130368 | bytes 3426536 | solution.py:44
  47.7 0.6 fusion.181
  49.0 0.6 fusion.181
  49.7 0.8 copy.126
  50.6 13.4 %all_gather.13 = bf16[1024,128]{0,1:T(8,128)(2,1)S(1)} all-gather(bf16[128,128]{0,1:T(8,128)(2,1)S(1)} %copy.103), channel_id=1, replica_groups=mesh['tensor'=2,'context'=8,'dp'=2] {'context'}, dimensions={0}, use_global_device_ids=true | all-gather | bytes 294912 | tf_op jit(solution)/shard_map/all_gather | solution.py:96
  64.0 14.3 %all_gather.12 = bf16[1024,128]{1,0:T(8,128)(2,1)S(1)} all-gather(bf16[128,128]{1,0:T(8,128)(2,1)S(1)} %copy-done.6), channel_id=1, replica_groups=mesh['tensor'=2,'context'=8,'dp'=2] {'context'}, dimensions={0}, use_global_device_ids=true | all-gather | bytes 294912 | tf_op jit(solution)/shard_map/all_gather | solution.py:95
  78.6 2.5 %while.76 = (s32[]{:T(128)}, f32[4,128]{1,0:T(4,128)S(1)}, f32[4,128]{1,0:T(4,128)S(1)}, f32[128,4,128]{0,2,1:T(8,128)S(1)}, s32[8]{0:T(128)S(1)}, /*index=5*/s3...) while((s32[]{:T(128)}, f32[4,128]{1,0:T(4,128)S(1)}, ...), condition=%wide.region_5.6_spmd.clone, body=%wide.region_1.5_spmd.clone.sunk | while | flops 136876544 | bytes 4371175 | solution.py:44
  79.2 0.4 fusion.165
  80.4 0.4 fusion.165
  81.1 0.8 copy.125
  81.9 1.5 %fusion.103 = bf16[128,128]{1,0:T(8,128)(2,1)} fusion(f32[128,256]{1,0:T(8,128)} %reduce-scatter.2.cloned.1.call-done), kind=kLoop, calls=%fused_computation.179 | loop fusion | flops 32768 | bytes 98304 | tf_op jit(solution)/shard_map/convert_element_type | solution.py:146
  83.3 1.5 %slice.15 = bf16[128,128]{1,0:T(8,128)(2,1)} slice(f32[128,256]{1,0:T(8,128)} %reduce-scatter.2.cloned.1.call-done), slice={[0:128], [128:256]} | slice | bytes 65536 | tf_op jit(solution)/shard_map/slice | solution.py:145
  (107 shorter events, 8.2 us)
Async XLA Ops:
  7.2 74.7 %reduce-scatter.2.cloned.1.call-start = ((), (), s32[]{:S(2)}) async-start(), calls=%async_computation.1 | async-start | bytes 1179648 | tf_op jit(solution)/shard_map/reduce_scatter | solution.py:138
  7.2 0.7 copy-start.1
  8.0 16.1 %copy-start.5 = (bf16[128,128]{1,0:T(8,128)(2,1)S(1)}, bf16[128,128]{1,0:T(8,128)(2,1)}, u32[]{:S(2)}) copy-start(bf16[128,128]{1,0:T(8,128)(2,1)} %param.18) | copy-start | bytes 98308
  24.1 14.3 %copy-start.2 = (bf16[128,512]{1,0:T(8,128)(2,1)S(1)}, bf16[128,512]{1,0:T(8,128)(2,1)}, u32[]{:S(2)}) copy-start(bf16[128,512]{1,0:T(8,128)(2,1)} %param.16) | copy-start | bytes 393220
  38.7 2.5 %copy-start.3 = (bf16[128,512]{1,0:T(8,128)(2,1)S(1)}, bf16[128,512]{1,0:T(8,128)(2,1)}, u32[]{:S(2)}) copy-start(bf16[128,512]{1,0:T(8,128)(2,1)} %param.19) | copy-start | bytes 393220
  45.3 0.6 copy-start.8
  45.3 1.0 %copy-start = (f32[1024,256]{1,0:T(8,128)}, f32[1024,256]{1,0:T(8,128)S(1)}, u32[]{:S(2)}) copy-start(f32[1024,256]{1,0:T(8,128)S(1)} %get-tuple-element.1085) | copy-start | bytes 3145732
  46.5 0.7 copy-start.9
  49.7 0.8 copy-start.7
  50.6 13.4 %copy-start.6 = (bf16[128,128]{1,0:T(8,128)(2,1)S(1)}, bf16[128,128]{1,0:T(8,128)(2,1)}, u32[]{:S(2)}) copy-start(bf16[128,128]{1,0:T(8,128)(2,1)} %param.21) | copy-start | bytes 98308
  64.0 14.3 %copy-start.4 = (bf16[128,512]{1,0:T(8,128)(2,1)S(1)}, bf16[128,512]{1,0:T(8,128)(2,1)}, u32[]{:S(2)}) copy-start(bf16[128,512]{1,0:T(8,128)(2,1)} %param.20) | copy-start | bytes 393220
Sparse Core Ops, SparseCore 0:
  46.4 33.9 reduce-scatter.1
where the time goes:
time: 92 us; the launch traced here: 91.6 us
  blocking collectives  58.2 us (63%)
  between operations  14.3 us (16%)
  matrix products  6.95 us (8%)
  local copies, waits for them, and re-layouts  6.94 us (8%)
  other arithmetic  4.74 us (5%)
    all_gather x1, blocking collectives, on_device(): lax.all_gather(key_a, 'context', axis=0, tiled=True)  16.1 us
    all_gather x1, blocking collectives, on_device(): lax.all_gather(value_a, 'context', axis=0, tiled=True)  14.3 us
    all_gather x1, blocking collectives, on_device(): lax.all_gather(key_b, 'context', axis=0, tiled=True)  14.3 us
    all_gather x1, blocking collectives, on_device(): lax.all_gather(value_b, 'context', axis=0, tiled=True)  13.4 us
    unnamed x29, local copies, waits for them, and re-layouts  3.36 us
    dot_general x6, matrix products, scores_of(): jnp.einsum('rhd,nd->hrn', queries, keys, preferred_element_type=jnp.float32)  1.94 us
  transfers between devices with their start and end apart: 1, of which 0 were waited for; matrix products, arithmetic and copies ran while one was open for 7% of the time, Pallas kernels for 0%

commit v1 on v0

v1 whole, which is shorter than its diff:
```python
import functools

import jax
import jax.numpy as jnp
from jax import lax
from jax.experimental import pallas as pl
from jax.experimental.pallas import tpu as pltpu
from jax.sharding import PartitionSpec as P

LOW = -1e30
LOG2E = 1.4426950408889634
F32 = jnp.float32
BF16 = jnp.bfloat16


def dot_nt(a, b):
    return lax.dot_general(a, b, (((1,), (1,)), ((), ())), preferred_element_type=F32)


def dot_nn(a, b):
    return lax.dot_general(a, b, (((1,), (0,)), ((), ())), preferred_element_type=F32)


def dot_tn(a, b):
    return lax.dot_general(a, b, (((0,), (0,)), ((), ())), preferred_element_type=F32)


def groups(x, op):
    out = x[0:8]
    for i in range(8, x.shape[0], 8):
        out = op(out, x[i:i + 8])
    return out


def kernel(
    n, tok, heads, dim,
    owner, qa, ka, va, ga, qb, kb, vb,
    out_b, out_dq, out_dk, out_dv,
    kv, q_a, g_a, q_b, scores, pgrad, top, tot, dsum, acc_t, res_q, res_b, res_kv,
    own, pair_out, pair_in, far_out, far_in,
    load_sem, store_sem, recv_sem, right_sem, left_sem, mate_sem,
    pair_send, pair_recv, far_send, far_recv,
):
    chips = n // 2
    me = lax.axis_index("context")
    chip, core = me // 2, me % 2
    mate = chip * 2 + (1 - core)
    rows = heads * tok
    half = tok // 2
    scale = dim ** (-0.5)
    factor = scale * LOG2E

    def to(idx):
        return dict(device_id={"context": idx}, device_id_type=pl.DeviceIdType.MESH)

    def kv_load(b, j):
        src = ((ka, va), (kb, vb))[b][j]
        return pltpu.make_async_copy(src, kv.at[b, me, j], load_sem.at[b * 2 + j])

    def head_load(i, h):
        src, dst = ((qa, q_a), (ga, g_a), (qb, q_b))[i]
        return pltpu.make_async_copy(
            src.at[:, pl.ds(h * dim, dim)], dst.at[pl.ds(h * tok, tok), :],
            load_sem.at[4 + i * heads + h],
        )

    for b in range(2):
        for j in range(2):
            kv_load(b, j).start()
    for i in range(3):
        for h in range(heads):
            head_load(i, h).start()

    barrier = pltpu.get_barrier_semaphore()
    for off in range(1, chips):
        pl.semaphore_signal(barrier, inc=1, **to(lax.rem(chip + off, chips) * 2 + core))
    pl.semaphore_signal(barrier, inc=1, **to(mate))
    for b in range(2):
        for j in range(2):
            kv_load(b, j).wait()
    pl.semaphore_wait(barrier, chips)

    def hop(b, slot, j, target, sems):
        return pltpu.make_async_remote_copy(
            src_ref=kv.at[b, slot, j], dst_ref=kv.at[b, slot, j],
            send_sem=sems.at[b, slot, j], recv_sem=recv_sem.at[b, slot, j], **to(target),
        )

    def go_right(b, slot, j):
        return hop(b, slot, j, jnp.minimum(me + 2, n - 1), right_sem)

    def go_left(b, slot, j):
        return hop(b, slot, j, jnp.maximum(me - 2, 0), left_sem)

    def go_mate(b, slot, j):
        return hop(b, slot, j, mate, mate_sem)

    can_right = chip + 1 < chips
    can_left = chip > 0

    def spread_own(b):
        @pl.when(can_right)
        def _():
            for j in range(2):
                go_right(b, me, j).start()

        @pl.when(can_left)
        def _():
            for j in range(2):
                go_left(b, me, j).start()

        for j in range(2):
            go_mate(b, me, j).start()

    def relay(b, t):
        from_left = me - 2 * t
        from_right = me + 2 * t
        for j in range(2):
            @pl.when(chip - t >= 0)
            def _():
                slot = jnp.maximum(from_left, 0)
                hop(b, slot, j, mate, mate_sem).wait_recv()

                @pl.when(can_right)
                def _():
                    go_right(b, slot, j).start()
                go_mate(b, slot, j).start()

            @pl.when(chip + t < chips)
            def _():
                slot = jnp.minimum(from_right, n - 1)
                hop(b, slot, j, mate, mate_sem).wait_recv()

                @pl.when(can_left)
                def _():
                    go_left(b, slot, j).start()
                go_mate(b, slot, j).start()

    def take_mate(b, slot):
        for j in range(2):
            hop(b, slot, j, mate, mate_sem).wait_recv()

    spread_own(0)

    lane = lax.broadcasted_iota(jnp.int32, (1, rows), 1) % tok
    mine = owner[me]
    places = jnp.where(lane < half, mine * half + lane, (2 * n - 1 - mine) * half + lane - half)
    key_row = lax.broadcasted_iota(jnp.int32, (half, rows), 0)

    def masked(s, slot):
        o = owner[slot]
        first = jnp.where(key_row <= places - o * half, s[:half], LOW)
        second = jnp.where(key_row <= places - (2 * n - 1 - o) * half, s[half:], LOW)
        return first, second

    def score_block(b, slot, queries):
        first, second = masked(dot_nt(kv[b, slot, 0], queries[...]), slot)
        scores[slot, :half] = first
        scores[slot, half:] = second
        top[...] = jnp.maximum(
            top[...], jnp.maximum(groups(first, jnp.maximum), groups(second, jnp.maximum))
        )

    def first_a(slot):
        score_block(0, slot, q_a)
        pgrad[slot] = dot_nt(kv[0, slot, 1], g_a[...])

    for i in range(3):
        for h in range(heads):
            head_load(i, h).wait()
    top[...] = jnp.full_like(top, LOW)
    first_a(me)

    def gather_a(t, _):
        relay(0, t)

        @pl.when(chip - t >= 0)
        def _():
            first_a(jnp.maximum(me - 2 * t, 0))

        @pl.when(chip + t < chips)
        def _():
            first_a(jnp.minimum(me + 2 * t, n - 1))
        return 0

    lax.fori_loop(1, chips, gather_a, 0)
    spread_own(1)

    def mates_a(d, _):
        slot = 2 * d + 1 - core
        take_mate(0, slot)
        first_a(slot)
        return 0

    lax.fori_loop(0, chips, mates_a, 0)

    peak = jnp.max(top[...], axis=0, keepdims=True) * factor
    tot[...] = jnp.zeros_like(tot)
    dsum[...] = jnp.zeros_like(dsum)

    def second_a(i, _):
        p = jnp.exp2(scores[i] * factor - peak)
        scores[i] = p
        tot[...] += groups(p, jnp.add)
        dsum[...] += groups(p * pgrad[i], jnp.add)
        return 0

    lax.fori_loop(0, n, second_a, 0)
    inv = 1.0 / jnp.sum(tot[...], axis=0, keepdims=True)
    delta = jnp.sum(dsum[...], axis=0, keepdims=True) * inv
    acc_t[...] = jnp.zeros_like(acc_t)

    def grads(slot):
        prob = scores[slot] * inv
        sg = (prob * (pgrad[slot] - delta)).astype(BF16)
        dk = dot_nn(sg, q_a[...])
        dv = dot_nn(prob.astype(BF16), g_a[...])
        acc_t[...] += dot_tn(kv[0, slot, 0], sg)
        return dk, dv

    def pair(d):
        return pltpu.make_async_remote_copy(
            src_ref=pair_out.at[d], dst_ref=pair_in.at[d],
            send_sem=pair_send.at[d], recv_sem=pair_recv.at[d], **to(mate),
        )

    def far(d):
        return pltpu.make_async_remote_copy(
            src_ref=far_out.at[d], dst_ref=far_in.at[chip],
            send_sem=far_send.at[d], recv_sem=far_recv.at[chip], **to(d * 2 + core),
        )

    def ship(d):
        pair(d).wait_recv()
        far_out[d] = (own[d] + pair_in[d].astype(F32)).astype(BF16)
        far(d).start()

    def third_a(t, _):
        @pl.when(t >= 1)
        def _():
            relay(1, t)
        d = lax.rem(chip + t + 1, chips)
        dk, dv = grads(2 * d + 1 - core)
        pair_out[d, 0] = dk.astype(BF16)
        pair_out[d, 1] = dv.astype(BF16)
        pair(d).start()
        dk, dv = grads(2 * d + core)
        own[d, 0] = dk
        own[d, 1] = dv

        @pl.when(t >= 1)
        def _():
            ship(lax.rem(chip + t, chips))
        return 0

    lax.fori_loop(0, chips, third_a, 0)

    def out_copy(i, h):
        src, dst = ((res_q, out_dq), (res_b, out_b))[i]
        return pltpu.make_async_copy(
            src.at[pl.ds(h * tok, tok), :], dst.at[:, pl.ds(h * dim, dim)],
            store_sem.at[i * heads + h],
        )

    res_q[...] = jnp.transpose(acc_t[...] * scale).astype(BF16)
    for h in range(heads):
        out_copy(0, h).start()

    top[...] = jnp.full_like(top, LOW)

    def take_b(d, _):
        take_mate(1, 2 * d + 1 - core)
        return 0

    lax.fori_loop(0, chips, take_b, 0)

    def first_b(i, _):
        score_block(1, i, q_b)
        return 0

    lax.fori_loop(0, n, first_b, 0)
    peak_b = jnp.max(top[...], axis=0, keepdims=True) * factor
    tot[...] = jnp.zeros_like(tot)
    acc_t[...] = jnp.zeros_like(acc_t)

    def second_b(i, _):
        p = jnp.exp2(scores[i] * factor - peak_b)
        tot[...] += groups(p, jnp.add)
        acc_t[...] += dot_tn(kv[1, i, 1], p.astype(BF16))
        return 0

    lax.fori_loop(0, n, second_b, 0)
    total_b = jnp.sum(tot[...], axis=0, keepdims=True)
    res_b[...] = jnp.transpose(acc_t[...] / total_b).astype(BF16)
    for h in range(heads):
        out_copy(1, h).start()

    pair(chip).wait_recv()
    own[chip] = own[chip] + pair_in[chip].astype(F32)

    def gather_sum(off, _):
        d = lax.rem(chip + off, chips)
        pltpu.make_async_remote_copy(
            src_ref=far_out.at[d], dst_ref=far_in.at[d],
            send_sem=far_send.at[d], recv_sem=far_recv.at[d], **to(d * 2 + core),
        ).wait_recv()
        own[chip] = own[chip] + far_in[d].astype(F32)
        return 0

    lax.fori_loop(1, chips, gather_sum, 0)
    res_kv[0] = (own[chip, 0] * scale).astype(BF16)
    res_kv[1] = own[chip, 1].astype(BF16)
    kv_out = [
        pltpu.make_async_copy(res_kv.at[j], (out_dk, out_dv)[j], store_sem.at[2 * heads + j])
        for j in range(2)
    ]
    for j in range(2):
        kv_out[j].start()

    def drain_far(off, _):
        far(lax.rem(chip + off, chips)).wait_send()
        return 0

    lax.fori_loop(1, chips, drain_far, 0)

    def drain(d, _):
        pair(d).wait_send()
        slot = 2 * d + core
        for b in range(2):
            for j in range(2):
                go_mate(b, slot, j).wait_send()

                @pl.when(jnp.logical_and(can_right, d <= chip))
                def _():
                    go_right(b, slot, j).wait_send()

                @pl.when(jnp.logical_and(can_left, d >= chip))
                def _():
                    go_left(b, slot, j).wait_send()
        return 0

    lax.fori_loop(0, chips, drain, 0)
    for i in range(2):
        for h in range(heads):
            out_copy(i, h).wait()
    for j in range(2):
        kv_out[j].wait()


def on_device(n, qa, ka, va, ga, qb, kb, vb, owner):
    tok, dim = ka.shape
    heads = qa.shape[1] // dim
    rows = heads * tok
    chips = n // 2
    any_spec = pl.BlockSpec(memory_space=pl.ANY)
    sem = pltpu.SemaphoreType.DMA
    return pl.pallas_call(
        functools.partial(kernel, n, tok, heads, dim),
        out_shape=(
            jax.ShapeDtypeStruct(qb.shape, BF16),
            jax.ShapeDtypeStruct(qa.shape, BF16),
            jax.ShapeDtypeStruct(ka.shape, BF16),
            jax.ShapeDtypeStruct(va.shape, BF16),
        ),
        in_specs=[pl.BlockSpec(memory_space=pltpu.SMEM)] + [any_spec] * 7,
        out_specs=(any_spec,) * 4,
        scratch_shapes=[
            pltpu.VMEM((2, n, 2, tok, dim), BF16),
            pltpu.VMEM((rows, dim), BF16),
            pltpu.VMEM((rows, dim), BF16),
            pltpu.VMEM((rows, dim), BF16),
            pltpu.VMEM((n, tok, rows), F32),
            pltpu.VMEM((n, tok, rows), F32),
            pltpu.VMEM((8, rows), F32),
            pltpu.VMEM((8, rows), F32),
            pltpu.VMEM((8, rows), F32),
            pltpu.VMEM((dim, rows), F32),
            pltpu.VMEM((rows, dim), BF16),
            pltpu.VMEM((rows, dim), BF16),
            pltpu.VMEM((2, tok, dim), BF16),
            pltpu.VMEM((chips, 2, tok, dim), F32),
            pltpu.VMEM((chips, 2, tok, dim), BF16),
            pltpu.VMEM((chips, 2, tok, dim), BF16),
            pltpu.VMEM((chips, 2, tok, dim), BF16),
            pltpu.VMEM((chips, 2, tok, dim), BF16),
            sem((4 + 3 * heads,)),
            sem((2 * heads + 2,)),
            sem((2, n, 2)),
            sem((2, n, 2)),
            sem((2, n, 2)),
            sem((2, n, 2)),
            sem((chips,)),
            sem((chips,)),
            sem((chips,)),
            sem((chips,)),
        ],
        compiler_params=pltpu.CompilerParams(collective_id=0, has_side_effects=True),
    )(owner, qa, ka, va, ga, qb, kb, vb)


def solution(mesh):
    spec = P(("dp", "context"), "tensor")
    return jax.shard_map(
        functools.partial(on_device, mesh.shape["context"]),
        mesh=mesh,
        in_specs=(spec,) * 7 + (P(),),
        out_specs=(spec,) * 4,
        check_vma=False,
    )
```

time: 92 us -> 37.8 us (0.41)
  blocking collectives: 58.2 us -> 0 us
  Pallas kernels: 0 us -> 33 us
  between operations: 14.3 us -> 0.65 us
  matrix products: 6.95 us -> 0 us
  other arithmetic: 4.74 us -> 0 us
  local copies, waits for them, and re-layouts: 6.94 us -> 3.75 us
    all_gather x4 -> x0, blocking collectives: 58.2 us -> none  [the longest x1 16.1 us: on_device(): lax.all_gather(key_a, 'context', axis=0, tiled=True)]
    pallas_call x0 -> x1, Pallas kernels: none -> 33 us  [on_device(): pl.pallas_call(functools.partial(kernel, n, tok, heads, dim), out_shape=(...]
    dot_general x18 -> x0, matrix products: 6.95 us -> none  [the longest x6 1.94 us: scores_of(): jnp.einsum('rhd,nd->hrn', queries, keys, preferred_element_type=jnp.float32)]
    reduce_sum x14 -> x0, other arithmetic: 1.65 us -> none  [the longest x4 0.83 us: attend(): total = total * factor + jnp.sum(raised, axis=2)]
    convert_element_type x2 -> x0, local copies, waits for them, and re-layouts: 1.54 us -> none  [the longest x1 0.77 us: on_device(): (query_sum * scale).reshape(tok_rows, heads * head_dim).astype(jnp.bfloat16)]
    convert_element_type x3 -> x0, other arithmetic: 1.52 us -> none  [the longest x1 1.46 us: on_device(): grad_key_a = (key_sum * scale).astype(jnp.bfloat16)]
    slice x1 -> x0, local copies, waits for them, and re-layouts: 1.46 us -> none  [on_device(): value_sum = terms[:, head_dim:]]
    le x8 -> x0, other arithmetic: 1.09 us -> none  [scores_of(): allowed = key_places[None, None, :] <= query_places[None, :, None]]
  transfers between devices with their start and end apart: 1 -> 0, of which waited for: 0 -> 0; matrix products, arithmetic and copies ran while one was open for 7% -> 0% of each run, Pallas kernels for 0% -> 0%
where the time goes in v1:
time: 37.8 us; the launch traced here: 37.4 us
  Pallas kernels  33 us (87%)
  local copies, waits for them, and re-layouts  3.75 us (10%)
  between operations  0.65 us (2%)
    pallas_call x1, Pallas kernels, on_device(): pl.pallas_call(functools.partial(kernel, n, tok, heads, dim), out_shape=(...  33 us
    unnamed x10, local copies, waits for them, and re-layouts  3.75 us

profile of v1, /device:TPU:0, one launch (start us, length us, event | category | flops | bytes accessed | tf_op | source)
XLA Modules:
  0.0 37.4 jit_solution(12725144610264732449)
XLA Ops:
  0.6 33.0 %shard_map.111 = (bf16[128,512]{1,0:T(8,128)(2,1)}, bf16[128,512]{1,0:T(8,128)(2,1)}, bf16[128,128]{1,0:T(8,128)(2,1)}, bf16[128,128]{1,0:T(8,128)(2,1)}) custom-call(s32[8]{0:T(128)} %owner.1, bf16[128,512]{1,0:T(8,128)(2,1)} %qa.1, bf16[128,128]{1,0:T(8,128)(2,1)} %ka.1, bf16[128,128]{1,0:T(8,128)(2,1)} %va.1, bf16[128,512]{1,0:T(8,128)(2,1)} %ga.1, ...), custom_call_target="tpu_custom_call" | custom-call | tf_op jit(solution)/shard_map/pallas_call | solution.py:357
  33.6 0.0 copy-start
  33.6 1.6 %copy.16 = bf16[128,512]{1,0:T(8,128)(2,1)} copy(bf16[128,512]{1,0:T(8,128)(2,1)} %get-tuple-element.8) | data formatting | bytes 262144
  35.2 0.0 copy-done
  35.2 0.0 copy-start.2
  35.2 0.7 %copy.17 = bf16[128,512]{1,0:T(8,128)(2,1)} copy(bf16[128,512]{1,0:T(8,128)(2,1)S(1)} %copy-done) | data formatting | bytes 262144
  35.9 0.1 copy-done.2
  36.0 0.0 copy-start.1
  36.0 0.6 %copy.18 = bf16[128,128]{1,0:T(8,128)(2,1)} copy(bf16[128,128]{1,0:T(8,128)(2,1)S(1)} %copy-done.2) | data formatting | bytes 65536
  36.6 0.2 copy-done.1
  36.8 0.6 %copy.19 = bf16[128,128]{1,0:T(8,128)(2,1)} copy(bf16[128,128]{1,0:T(8,128)(2,1)S(1)} %copy-done.1) | data formatting | bytes 65536
Async XLA Ops:
  33.6 1.6 %copy-start = (bf16[128,512]{1,0:T(8,128)(2,1)S(1)}, bf16[128,512]{1,0:T(8,128)(2,1)}, u32[]{:S(2)}) copy-start(bf16[128,512]{1,0:T(8,128)(2,1)} %get-tuple-element.9) | copy-start | bytes 393220
  35.2 0.8 %copy-start.2 = (bf16[128,128]{1,0:T(8,128)(2,1)S(1)}, bf16[128,128]{1,0:T(8,128)(2,1)}, u32[]{:S(2)}) copy-start(bf16[128,128]{1,0:T(8,128)(2,1)} %get-tuple-element.10) | copy-start | bytes 98308
  36.0 0.8 %copy-start.1 = (bf16[128,128]{1,0:T(8,128)(2,1)S(1)}, bf16[128,128]{1,0:T(8,128)(2,1)}, u32[]{:S(2)}) copy-start(bf16[128,128]{1,0:T(8,128)(2,1)} %get-tuple-element.11) | copy-start | bytes 98308

commit v2 on v1

--- a/solution.py
+++ b/solution.py
@@ -36,9 +36,9 @@
     n, tok, heads, dim,
     owner, qa, ka, va, ga, qb, kb, vb,
     out_b, out_dq, out_dk, out_dv,
-    kv, q_a, g_a, q_b, scores, pgrad, top, tot, dsum, acc_t, res_q, res_b, res_kv,
+    kv, q_a, g_a, q_b, scores, pgrad, top, tot, dsum, acc_t, both,
     own, pair_out, pair_in, far_out, far_in,
-    load_sem, store_sem, recv_sem, right_sem, left_sem, mate_sem,
+    load_sem, recv_sem, right_sem, left_sem, mate_sem,
     pair_send, pair_recv, far_send, far_recv,
 ):
     chips = n // 2
@@ -141,58 +141,63 @@
             hop(b, slot, j, mate, mate_sem).wait_recv()
 
     spread_own(0)
+    spread_own(1)
 
     lane = lax.broadcasted_iota(jnp.int32, (1, rows), 1) % tok
     mine = owner[me]
     places = jnp.where(lane < half, mine * half + lane, (2 * n - 1 - mine) * half + lane - half)
     key_row = lax.broadcasted_iota(jnp.int32, (half, rows), 0)
 
-    def masked(s, slot):
-        o = owner[slot]
-        first = jnp.where(key_row <= places - o * half, s[:half], LOW)
-        second = jnp.where(key_row <= places - (2 * n - 1 - o) * half, s[half:], LOW)
-        return first, second
-
-    def score_block(b, slot, queries):
-        first, second = masked(dot_nt(kv[b, slot, 0], queries[...]), slot)
-        scores[slot, :half] = first
-        scores[slot, half:] = second
-        top[...] = jnp.maximum(
-            top[...], jnp.maximum(groups(first, jnp.maximum), groups(second, jnp.maximum))
-        )
-
-    def first_a(slot):
-        score_block(0, slot, q_a)
-        pgrad[slot] = dot_nt(kv[0, slot, 1], g_a[...])
+    def score_pair(b, d, queries):
+        keys = kv[b, pl.ds(2 * d, 2), 0].reshape(2 * tok, dim)
+        raw = dot_nt(keys, queries[...])
+        best = top[...]
+        for c in range(2):
+            o = owner[2 * d + c]
+            for part, slab in ((0, o), (1, 2 * n - 1 - o)):
+                lo = c * tok + part * half
+                piece = jnp.where(key_row <= places - slab * half, raw[lo:lo + half], LOW)
+                scores[d, lo:lo + half] = piece
+                best = jnp.maximum(best, groups(piece, jnp.maximum))
+        top[...] = best
+
+    def first_a(d):
+        take_mate(0, 2 * d + 1 - core)
+        score_pair(0, d, q_a)
+        pgrad[d] = dot_nt(kv[0, pl.ds(2 * d, 2), 1].reshape(2 * tok, dim), g_a[...])
 
     for i in range(3):
         for h in range(heads):
             head_load(i, h).wait()
     top[...] = jnp.full_like(top, LOW)
-    first_a(me)
 
     def gather_a(t, _):
         relay(0, t)
 
-        @pl.when(chip - t >= 0)
-        def _():
-            first_a(jnp.maximum(me - 2 * t, 0))
-
-        @pl.when(chip + t < chips)
-        def _():
-            first_a(jnp.minimum(me + 2 * t, n - 1))
+        @pl.when(chip - t + 1 >= 0)
+        def _():
+            first_a(jnp.maximum(chip - t + 1, 0))
+
+        @pl.when(jnp.logical_and(chip + t - 1 < chips, t > 1))
+        def _():
+            first_a(jnp.minimum(chip + t - 1, chips - 1))
+
+        @pl.when(t < chips - 1)
+        def _():
+            relay(1, t)
         return 0
 
     lax.fori_loop(1, chips, gather_a, 0)
-    spread_own(1)
-
-    def mates_a(d, _):
-        slot = 2 * d + 1 - core
-        take_mate(0, slot)
-        first_a(slot)
-        return 0
-
-    lax.fori_loop(0, chips, mates_a, 0)
+
+    @pl.when(chip == chips - 1)
+    def _():
+        first_a(0)
+
+    @pl.when(chip == 0)
+    def _():
+        first_a(chips - 1)
+
+    relay(1, chips - 1)
 
     peak = jnp.max(top[...], axis=0, keepdims=True) * factor
     tot[...] = jnp.zeros_like(tot)
@@ -205,18 +210,17 @@
         dsum[...] += groups(p * pgrad[i], jnp.add)
         return 0
 
-    lax.fori_loop(0, n, second_a, 0)
+    lax.fori_loop(0, chips, second_a, 0)
     inv = 1.0 / jnp.sum(tot[...], axis=0, keepdims=True)
     delta = jnp.sum(dsum[...], axis=0, keepdims=True) * inv
     acc_t[...] = jnp.zeros_like(acc_t)
 
-    def grads(slot):
-        prob = scores[slot] * inv
-        sg = (prob * (pgrad[slot] - delta)).astype(BF16)
-        dk = dot_nn(sg, q_a[...])
-        dv = dot_nn(prob.astype(BF16), g_a[...])
-        acc_t[...] += dot_tn(kv[0, slot, 0], sg)
-        return dk, dv
+    def grads(d):
+        prob = scores[d] * inv
+        sg = (prob * (pgrad[d] - delta)).astype(BF16)
+        both[0] = dot_nn(sg, q_a[...]).reshape(2, tok, dim)
+        both[1] = dot_nn(prob.astype(BF16), g_a[...]).reshape(2, tok, dim)
+        acc_t[...] += dot_tn(kv[0, pl.ds(2 * d, 2), 0].reshape(2 * tok, dim), sg)
 
     def pair(d):
         return pltpu.make_async_remote_copy(
@@ -236,35 +240,27 @@
         far(d).start()
 
     def third_a(t, _):
+        d = lax.rem(chip + t + 1, chips)
+        grads(d)
+        for j in range(2):
+            pair_out[d, j] = both[j, 1 - core].astype(BF16)
+        pair(d).start()
+        for j in range(2):
+            own[d, j] = both[j, core]
+
         @pl.when(t >= 1)
         def _():
-            relay(1, t)
-        d = lax.rem(chip + t + 1, chips)
-        dk, dv = grads(2 * d + 1 - core)
-        pair_out[d, 0] = dk.astype(BF16)
-        pair_out[d, 1] = dv.astype(BF16)
-        pair(d).start()
-        dk, dv = grads(2 * d + core)
-        own[d, 0] = dk
-        own[d, 1] = dv
-
-        @pl.when(t >= 1)
-        def _():
             ship(lax.rem(chip + t, chips))
         return 0
 
     lax.fori_loop(0, chips, third_a, 0)
 
-    def out_copy(i, h):
-        src, dst = ((res_q, out_dq), (res_b, out_b))[i]
-        return pltpu.make_async_copy(
-            src.at[pl.ds(h * tok, tok), :], dst.at[:, pl.ds(h * dim, dim)],
-            store_sem.at[i * heads + h],
-        )
-
-    res_q[...] = jnp.transpose(acc_t[...] * scale).astype(BF16)
-    for h in range(heads):
-        out_copy(0, h).start()
+    def put(out, x):
+        low = jnp.transpose(x).astype(BF16)
+        for h in range(heads):
+            out[:, h * dim:(h + 1) * dim] = low[h * tok:(h + 1) * tok]
+
+    put(out_dq, acc_t[...] * scale)
 
     top[...] = jnp.full_like(top, LOW)
 
@@ -275,10 +271,10 @@
     lax.fori_loop(0, chips, take_b, 0)
 
     def first_b(i, _):
-        score_block(1, i, q_b)
-        return 0
-
-    lax.fori_loop(0, n, first_b, 0)
+        score_pair(1, i, q_b)
+        return 0
+
+    lax.fori_loop(0, chips, first_b, 0)
     peak_b = jnp.max(top[...], axis=0, keepdims=True) * factor
     tot[...] = jnp.zeros_like(tot)
     acc_t[...] = jnp.zeros_like(acc_t)
@@ -286,14 +282,12 @@
     def second_b(i, _):
         p = jnp.exp2(scores[i] * factor - peak_b)
         tot[...] += groups(p, jnp.add)
-        acc_t[...] += dot_tn(kv[1, i, 1], p.astype(BF16))
-        return 0
-
-    lax.fori_loop(0, n, second_b, 0)
+        acc_t[...] += dot_tn(kv[1, pl.ds(2 * i, 2), 1].reshape(2 * tok, dim), p.astype(BF16))
+        return 0
+
+    lax.fori_loop(0, chips, second_b, 0)
     total_b = jnp.sum(tot[...], axis=0, keepdims=True)
-    res_b[...] = jnp.transpose(acc_t[...] / total_b).astype(BF16)
-    for h in range(heads):
-        out_copy(1, h).start()
+    put(out_b, acc_t[...] / total_b)
 
     pair(chip).wait_recv()
     own[chip] = own[chip] + pair_in[chip].astype(F32)
@@ -308,14 +302,8 @@
         return 0
 
     lax.fori_loop(1, chips, gather_sum, 0)
-    res_kv[0] = (own[chip, 0] * scale).astype(BF16)
-    res_kv[1] = own[chip, 1].astype(BF16)
-    kv_out = [
-        pltpu.make_async_copy(res_kv.at[j], (out_dk, out_dv)[j], store_sem.at[2 * heads + j])
-        for j in range(2)
-    ]
-    for j in range(2):
-        kv_out[j].start()
+    out_dk[...] = (own[chip, 0] * scale).astype(BF16)
+    out_dv[...] = own[chip, 1].astype(BF16)
 
     def drain_far(off, _):
         far(lax.rem(chip + off, chips)).wait_send()
@@ -340,11 +328,18 @@
         return 0
 
     lax.fori_loop(0, chips, drain, 0)
-    for i in range(2):
-        for h in range(heads):
-            out_copy(i, h).wait()
-    for j in range(2):
-        kv_out[j].wait()
+
+
+def emit(*refs):
+    count = len(refs) // 2
+    sems = refs[-1]
+    copies = [
+        pltpu.make_async_copy(refs[i], refs[count + i], sems.at[i]) for i in range(count)
+    ]
+    for copy in copies:
+        copy.start()
+    for copy in copies:
+        copy.wait()
 
 
 def on_device(n, qa, ka, va, ga, qb, kb, vb, owner):
@@ -354,37 +349,35 @@
     chips = n // 2
     any_spec = pl.BlockSpec(memory_space=pl.ANY)
     sem = pltpu.SemaphoreType.DMA
-    return pl.pallas_call(
+    vmem_spec = pl.BlockSpec(memory_space=pltpu.VMEM)
+    outs = pl.pallas_call(
         functools.partial(kernel, n, tok, heads, dim),
         out_shape=(
-            jax.ShapeDtypeStruct(qb.shape, BF16),
-            jax.ShapeDtypeStruct(qa.shape, BF16),
-            jax.ShapeDtypeStruct(ka.shape, BF16),
-            jax.ShapeDtypeStruct(va.shape, BF16),
+            pltpu.VMEM(qb.shape, BF16),
+            pltpu.VMEM(qa.shape, BF16),
+            pltpu.VMEM(ka.shape, BF16),
+            pltpu.VMEM(va.shape, BF16),
         ),
         in_specs=[pl.BlockSpec(memory_space=pltpu.SMEM)] + [any_spec] * 7,
-        out_specs=(any_spec,) * 4,
+        out_specs=(vmem_spec,) * 4,
         scratch_shapes=[
             pltpu.VMEM((2, n, 2, tok, dim), BF16),
             pltpu.VMEM((rows, dim), BF16),
             pltpu.VMEM((rows, dim), BF16),
             pltpu.VMEM((rows, dim), BF16),
-            pltpu.VMEM((n, tok, rows), F32),
-            pltpu.VMEM((n, tok, rows), F32),
+            pltpu.VMEM((chips, 2 * tok, rows), F32),
+            pltpu.VMEM((chips, 2 * tok, rows), F32),
             pltpu.VMEM((8, rows), F32),
             pltpu.VMEM((8, rows), F32),
             pltpu.VMEM((8, rows), F32),
             pltpu.VMEM((dim, rows), F32),
-            pltpu.VMEM((rows, dim), BF16),
-            pltpu.VMEM((rows, dim), BF16),
-            pltpu.VMEM((2, tok, dim), BF16),
+            pltpu.VMEM((2, 2, tok, dim), F32),
             pltpu.VMEM((chips, 2, tok, dim), F32),
             pltpu.VMEM((chips, 2, tok, dim), BF16),
             pltpu.VMEM((chips, 2, tok, dim), BF16),
             pltpu.VMEM((chips, 2, tok, dim), BF16),
             pltpu.VMEM((chips, 2, tok, dim), BF16),
             sem((4 + 3 * heads,)),
-            sem((2 * heads + 2,)),
             sem((2, n, 2)),
             sem((2, n, 2)),
             sem((2, n, 2)),
@@ -396,6 +389,14 @@
         ],
         compiler_params=pltpu.CompilerParams(collective_id=0, has_side_effects=True),
     )(owner, qa, ka, va, ga, qb, kb, vb)
+    return pl.pallas_call(
+        emit,
+        out_shape=tuple(jax.ShapeDtypeStruct(x.shape, x.dtype) for x in outs),
+        in_specs=[vmem_spec] * 4,
+        out_specs=(any_spec,) * 4,
+        scratch_shapes=[sem((4,))],
+        compiler_params=pltpu.CompilerParams(vmem_limit_bytes=8 * 2**20),
+    )(*outs)
 
 
 def solution(mesh):

time: 37.8 us -> 26.3 us (0.70)
  Pallas kernels: 33 us -> 25.5 us
  local copies, waits for them, and re-layouts: 3.75 us -> 0 us
    pallas_call x1, Pallas kernels: 33 us -> 24.7 us  [on_device(): pl.pallas_call(functools.partial(kernel, n, tok, heads, dim), out_shape=(...]
    unnamed x10 -> x0, local copies, waits for them, and re-layouts: 3.75 us -> none
    pallas_call x0 -> x1, Pallas kernels: none -> 0.75 us  [on_device(): pl.pallas_call(emit, out_shape=tuple((jax.ShapeDtypeStruct(x.shape, x.dty...]
where the time goes in v2:
time: 26.3 us; the launch traced here: 26.1 us
  Pallas kernels  25.5 us (97%)
  between operations  0.64 us (2%)
    pallas_call x1, Pallas kernels, on_device(): pl.pallas_call(functools.partial(kernel, n, tok, heads, dim), out_shape=(...  24.7 us
    pallas_call x1, Pallas kernels, on_device(): pl.pallas_call(emit, out_shape=tuple((jax.ShapeDtypeStruct(x.shape, x.dty...  0.75 us

profile of v2, /device:TPU:0, one launch (start us, length us, event | category | flops | bytes accessed | tf_op | source)
XLA Modules:
  0.0 26.1 jit_solution(4236489964123974483)
XLA Ops:
  0.6 24.7 %shard_map.111 = (bf16[128,512]{1,0:T(8,128)(2,1)S(1)}, bf16[128,512]{1,0:T(8,128)(2,1)S(1)}, bf16[128,128]{1,0:T(8,128)(2,1)S(1)}, bf16[128,128]{1,0:T(8,128)(2,1)S(1)}) custom-call(s32[8]{0:T(128)} %owner.1, bf16[128,512]{1,0:T(8,128)(2,1)} %qa.1, bf16[128,128]{1,0:T(8,128)(2,1)} %ka.1, bf16[128,128]{1,0:T(8,128)(2,1)} %va.1, bf16[128,512]{1,0:T(8,128)(2,1)} %ga.1, ...), custom_call_target="tpu_custom_call" | custom-call | tf_op jit(solution)/shard_map/pallas_call | solution.py:353
  25.4 0.7 %shard_map.112 = (bf16[128,512]{1,0:T(8,128)(2,1)}, bf16[128,512]{1,0:T(8,128)(2,1)}, bf16[128,128]{1,0:T(8,128)(2,1)}, bf16[128,128]{1,0:T(8,128)(2,1)}) custom-call(bf16[128,512]{1,0:T(8,128)(2,1)S(1)} %get-tuple-element.8.refs_0_, bf16[128,512]{1,0:T(8,128)(2,1)S(1)} %get-tuple-element.9.refs_1_, bf16[128,128]{1,0:T(8,128)(2,1)S(1)} %get-tuple-element.10.refs_2_, ...), custom_call_target="tpu_custom_call" | custom-call | tf_op jit(solution)/shard_map/pallas_call | solution.py:392

commit v3 on v2

--- a/solution.py
+++ b/solution.py
@@ -121,9 +121,10 @@
                 slot = jnp.maximum(from_left, 0)
                 hop(b, slot, j, mate, mate_sem).wait_recv()
 
-                @pl.when(can_right)
-                def _():
-                    go_right(b, slot, j).start()
+                if b == 1:
+                    @pl.when(can_right)
+                    def _():
+                        go_right(b, slot, j).start()
                 go_mate(b, slot, j).start()
 
             @pl.when(chip + t < chips)
@@ -131,16 +132,33 @@
                 slot = jnp.minimum(from_right, n - 1)
                 hop(b, slot, j, mate, mate_sem).wait_recv()
 
-                @pl.when(can_left)
-                def _():
-                    go_left(b, slot, j).start()
+                if b == 1:
+                    @pl.when(can_left)
+                    def _():
+                        go_left(b, slot, j).start()
                 go_mate(b, slot, j).start()
 
     def take_mate(b, slot):
         for j in range(2):
             hop(b, slot, j, mate, mate_sem).wait_recv()
 
-    spread_own(0)
+    def direct(d, j):
+        return pltpu.make_async_remote_copy(
+            src_ref=kv.at[0, me, j], dst_ref=kv.at[0, me, j],
+            send_sem=right_sem.at[0, d, j], recv_sem=recv_sem.at[0, me, j], **to(2 * d + core),
+        )
+
+    for j in range(2):
+        go_mate(0, me, j).start()
+    for t in range(chips - 1, 0, -1):
+        for j in range(2):
+            @pl.when(chip + t < chips)
+            def _():
+                direct(jnp.minimum(chip + t, chips - 1), j).start()
+
+            @pl.when(chip - t >= 0)
+            def _():
+                direct(jnp.maximum(chip - t, 0), j).start()
     spread_own(1)
 
     lane = lax.broadcasted_iota(jnp.int32, (1, rows), 1) % tok
@@ -317,6 +335,11 @@
         for b in range(2):
             for j in range(2):
                 go_mate(b, slot, j).wait_send()
+                if b == 0:
+                    @pl.when(d != chip)
+                    def _():
+                        direct(d, j).wait_send()
+                    continue
 
                 @pl.when(jnp.logical_and(can_right, d <= chip))
                 def _():

time: 26.3 us -> 29.1 us (1.11)
  Pallas kernels: 25.5 us -> 28.2 us
    pallas_call x1, Pallas kernels: 24.7 us -> 27.5 us  [on_device(): pl.pallas_call(functools.partial(kernel, n, tok, heads, dim), out_shape=(...]
where the time goes in v3:
time: 29.1 us; the launch traced here: 28.9 us
  Pallas kernels  28.2 us (97%)
  between operations  0.64 us (2%)
    pallas_call x1, Pallas kernels, on_device(): pl.pallas_call(functools.partial(kernel, n, tok, heads, dim), out_shape=(...  27.5 us
    pallas_call x1, Pallas kernels, on_device(): pl.pallas_call(emit, out_shape=tuple((jax.ShapeDtypeStruct(x.shape, x.dty...  0.75 us

profile of v3, /device:TPU:0, one launch (start us, length us, event | category | flops | bytes accessed | tf_op | source)
XLA Modules:
  0.0 28.9 jit_solution(3641454562148105568)
XLA Ops:
  0.6 27.5 %shard_map.111 = (bf16[128,512]{1,0:T(8,128)(2,1)S(1)}, bf16[128,512]{1,0:T(8,128)(2,1)S(1)}, bf16[128,128]{1,0:T(8,128)(2,1)S(1)}, bf16[128,128]{1,0:T(8,128)(2,1)S(1)}) custom-call(s32[8]{0:T(128)} %owner.1, bf16[128,512]{1,0:T(8,128)(2,1)} %qa.1, bf16[128,128]{1,0:T(8,128)(2,1)} %ka.1, bf16[128,128]{1,0:T(8,128)(2,1)} %va.1, bf16[128,512]{1,0:T(8,128)(2,1)} %ga.1, ...), custom_call_target="tpu_custom_call" | custom-call | tf_op jit(solution)/shard_map/pallas_call | solution.py:376
  28.1 0.7 %shard_map.112 = (bf16[128,512]{1,0:T(8,128)(2,1)}, bf16[128,512]{1,0:T(8,128)(2,1)}, bf16[128,128]{1,0:T(8,128)(2,1)}, bf16[128,128]{1,0:T(8,128)(2,1)}) custom-call(bf16[128,512]{1,0:T(8,128)(2,1)S(1)} %get-tuple-element.8.refs_0_, bf16[128,512]{1,0:T(8,128)(2,1)S(1)} %get-tuple-element.9.refs_1_, bf16[128,128]{1,0:T(8,128)(2,1)S(1)} %get-tuple-element.10.refs_2_, ...), custom_call_target="tpu_custom_call" | custom-call | tf_op jit(solution)/shard_map/pallas_call | solution.py:415
